TPU v7x, 32 devices: a whole 2x2x4 slice. The times are simulated.
32 devices in a mesh: patch: 16 (over z, y, x), pix: 2 (over core).
Axes of the slice: x: 2, y: 2, z: 4, core: 2. Of those that a mesh axis runs over, the one named last changes fastest.
Arguments:
- pixel_pos: float32 [2, 3072], P(None, ('patch', 'pix')), may hold values from -4 to 4
- pixel_view: float32 [3, 3072], P(None, ('patch', 'pix')), may hold values from -1 to 1
- observed: float32 [3072], P(('patch', 'pix')), may hold values from -6 to 6
- noise_scale: float32 [3072], P(('patch', 'pix')), may hold values from 0.5 to 2
- valid_mask: int32 [3072], P(('patch', 'pix')), may hold values 0 or 1
- patch_pos: float32 [2, 768], P(None, 'patch'), may hold values from -4 to 4
- patch_depth: float32 [768], P('patch'), may hold values from 0.3 to 1.5
- segment_ids: int32 [768], P('patch'), may hold values from 0 to 15, never falling along the last dimension, each value on 1 to 192 neighbouring positions
- seg_strike: float32 [16], replicated, may hold values from -3.140625 to 3.140625
- seg_dip: float32 [16], replicated, may hold values from 0.35 to 1.4
- slip_models: bfloat16 [768, 3, 128], P('patch'), may hold values from -0.8984375 to 0.8984375
Outputs:
- residual: float32 [3072, 128], P(('patch', 'pix'))
- misfit: float32 [128], replicated
Inputs may be any that keep to these rules, and one draw needn't show every extreme that they name: `segment_ids`: segment ids never fall along the patches.
All inputs are finite; a program needn't handle non-finite values. No bound on the sum of `valid_mask` on one device may be relied on, other than what follows from the above.
Results may differ from a plain program's by a relative error of at most 0.0003.
Values may be sent and summed in bfloat16 or wider, within the bound.
A program may use at most 64 MiB of HBM per device.

v0:
```python
import math

import jax
import jax.numpy as jnp
from jax import lax
from jax.sharding import PartitionSpec as P

two_pi = 2.0 * math.pi
mu_ratio = 0.5


def partner(value, axis, distance):
    mask = 2**distance
    pairs = [(source, source ^ mask) for source in range(lax.axis_size(axis))]
    return lax.ppermute(value, axis, pairs)


def point_green(pixel_pos, pixel_view, frame_rows):
    src_east = frame_rows[0][:, None]
    src_north = frame_rows[1][:, None]
    src_depth = frame_rows[2][:, None]
    sin_strike = frame_rows[3][:, None]
    cos_strike = frame_rows[4][:, None]
    sin_dip = frame_rows[5][:, None]
    cos_dip = frame_rows[6][:, None]
    east_gap = pixel_pos[0][None, :] - src_east
    north_gap = pixel_pos[1][None, :] - src_north
    along_x = east_gap * sin_strike + north_gap * cos_strike
    across = north_gap * sin_strike - east_gap * cos_strike
    depth_term = across * cos_dip + src_depth * sin_dip
    plane_term = across * sin_dip - src_depth * cos_dip
    radius = jnp.sqrt(along_x * along_x + across * across + src_depth * src_depth)
    over_r = 1.0 / radius
    over_r3 = over_r * over_r * over_r
    over_r5 = over_r3 * over_r * over_r
    over_rd = 1.0 / (radius + src_depth)
    base_term = over_r * over_rd * over_rd
    cubic_term = (3.0 * radius + src_depth) * over_r3 * over_rd * over_rd * over_rd
    square_term = (2.0 * radius + src_depth) * over_r3 * over_rd * over_rd
    term_one = mu_ratio * across * (base_term - along_x * along_x * cubic_term)
    term_two = mu_ratio * along_x * (base_term - across * across * cubic_term)
    term_three = mu_ratio * along_x * over_r3 - term_two
    term_four = -mu_ratio * along_x * across * square_term
    term_five = mu_ratio * (over_r * over_rd - along_x * along_x * square_term)
    scaled_q = 3.0 * plane_term * over_r5
    dip_mixed = sin_dip * cos_dip
    dip_square = sin_dip * sin_dip
    strike_x = -(scaled_q * along_x * along_x + term_one * sin_dip)
    strike_y = -(scaled_q * along_x * across + term_two * sin_dip)
    strike_z = -(scaled_q * along_x * src_depth + term_four * sin_dip)
    dip_x = -(scaled_q * along_x * depth_term - term_three * dip_mixed)
    dip_y = -(scaled_q * across * depth_term - term_one * dip_mixed)
    dip_z = -(scaled_q * src_depth * depth_term - term_five * dip_mixed)
    open_x = scaled_q * along_x * plane_term - term_three * dip_square
    open_y = scaled_q * across * plane_term - term_one * dip_square
    open_z = scaled_q * src_depth * plane_term - term_five * dip_square

    def project(comp_x, comp_y, comp_z):
        east_move = comp_x * sin_strike - comp_y * cos_strike
        north_move = comp_x * cos_strike + comp_y * sin_strike
        return (
            pixel_view[0][None, :] * east_move
            + pixel_view[1][None, :] * north_move
            + pixel_view[2][None, :] * comp_z
        ) / two_pi

    return jnp.stack(
        [
            project(strike_x, strike_y, strike_z),
            project(dip_x, dip_y, dip_z),
            project(open_x, open_y, open_z),
        ],
        axis=1,
    )


def local_frames(patch_pos, patch_depth, segment_ids, seg_strike, seg_dip):
    segment_count = seg_strike.shape[0]
    matches = segment_ids[:, None] == jnp.arange(segment_count, dtype=jnp.int32)[None, :]
    strike = jnp.sum(jnp.where(matches, seg_strike[None, :], 0.0), axis=1)
    dip_angle = jnp.sum(jnp.where(matches, seg_dip[None, :], 0.0), axis=1)
    return jnp.stack(
        [
            patch_pos[0],
            patch_pos[1],
            patch_depth,
            jnp.sin(strike),
            jnp.cos(strike),
            jnp.sin(dip_angle),
            jnp.cos(dip_angle),
        ],
        axis=0,
    )


def tile_product(site_pos, site_view, frame_rows, slip_table):
    pixel_count = site_pos.shape[1]
    green_tile = point_green(site_pos, site_view, frame_rows).astype(jnp.bfloat16)
    green_tile = green_tile.reshape(frame_rows.shape[1] * 3, pixel_count)
    return lax.dot_general(
        green_tile, slip_table, (((0,), (0,)), ((), ())), preferred_element_type=jnp.float32
    )


def patch_blocks(pixel_pos, pixel_view, frame_rows, slip_piece, running):
    patch_count = slip_piece.shape[0]
    samples = slip_piece.shape[2]
    block_len = min(patch_count, 640)
    full_blocks = patch_count // block_len
    remainder = patch_count - full_blocks * block_len
    head = full_blocks * block_len
    head_frames = frame_rows[:, :head].reshape(7, full_blocks, block_len).transpose(1, 0, 2)
    head_slip = slip_piece[:head].reshape(full_blocks, block_len * 3, samples)

    def add_tile(accum, block_items):
        return (accum + tile_product(pixel_pos, pixel_view, block_items[0], block_items[1]), None)

    running, _ = lax.scan(add_tile, running, (head_frames, head_slip))
    if remainder > 0:
        tail_slip = slip_piece[head:].reshape(remainder * 3, samples)
        running = running + tile_product(pixel_pos, pixel_view, frame_rows[:, head:], tail_slip)
    return running


def index_bit(level):
    return lax.axis_index("patch") // 2**level % 2 == 1


def join_pair(mine, other, upper, axis_dim):
    first = jnp.where(upper, other, mine)
    second = jnp.where(upper, mine, other)
    return jnp.concatenate([first, second], axis=axis_dim)


def per_device(
    pixel_pos,
    pixel_view,
    observed,
    noise_scale,
    valid_mask,
    patch_pos,
    patch_depth,
    segment_ids,
    seg_strike,
    seg_dip,
    slip_models,
):
    own_pixels = pixel_pos.shape[1]
    samples = slip_models.shape[2]
    frames = local_frames(patch_pos, patch_depth, segment_ids, seg_strike, seg_dip)
    total_bits = lax.axis_size("patch").bit_length() - 1
    low_count = (total_bits + 1) // 2
    group_slip = slip_models
    group_frames = frames
    for level in range(low_count):
        upper = index_bit(level)
        other_slip = partner(group_slip, "patch", level)
        other_frames = partner(group_frames, "patch", level)
        group_slip = join_pair(group_slip, other_slip, upper, 0)
        group_frames = join_pair(group_frames, other_frames, upper, 1)
    group_sites = jnp.concatenate([pixel_pos, pixel_view], axis=0)
    for level in range(low_count, total_bits):
        upper = index_bit(level)
        other_sites = partner(group_sites, "patch", level)
        group_sites = join_pair(group_sites, other_sites, upper, 1)
    site_groups = group_sites.shape[1] // own_pixels
    stacked = group_sites.reshape(5, site_groups, own_pixels).transpose(1, 0, 2)

    def one_group(block_sites):
        start = jnp.zeros((own_pixels, samples), jnp.float32)
        return patch_blocks(block_sites[:2], block_sites[2:], group_frames, group_slip, start)

    partial_value = lax.map(one_group, stacked).reshape(site_groups * own_pixels, samples)
    for level in range(total_bits - 1, low_count - 1, -1):
        upper = index_bit(level)
        half = partial_value.shape[0] // 2
        keep = jnp.where(upper, partial_value[half:], partial_value[:half])
        send = jnp.where(upper, partial_value[:half], partial_value[half:])
        partial_value = keep + partner(send, "patch", level)
    residual = (
        valid_mask.astype(jnp.float32)[:, None]
        * (partial_value - observed[:, None])
        / noise_scale[:, None]
    )
    own_sum = jnp.sum(residual * residual, axis=0)
    pixels = own_pixels * lax.axis_size("patch") * lax.axis_size("pix")
    misfit = lax.psum(own_sum, ("patch", "pix")) / pixels
    return (residual, misfit)


def solution(mesh):
    return jax.shard_map(
        per_device,
        mesh=mesh,
        in_specs=(
            P(None, ("patch", "pix")),
            P(None, ("patch", "pix")),
            P(("patch", "pix")),
            P(("patch", "pix")),
            P(("patch", "pix")),
            P(None, "patch"),
            P("patch"),
            P("patch"),
            P(),
            P(),
            P("patch", None, None),
        ),
        out_specs=(P(("patch", "pix"), None), P()),
        check_vma=False,
    )
```

profile of v0, /device:TPU:0, one launch (start us, length us, event | category | flops | bytes accessed | tf_op | source)
XLA Modules:
  0.0 74.1 jit_solution(12593632684655895281)
XLA Ops:
  0.6 3.0 %collective-permute-start.4 = (bf16[48,3,128]{2,0,1:T(8,128)(2,1)}, bf16[48,3,128]{2,0,1:T(8,128)(2,1)S(1)}, u32[]{:S(2)}, u32[]{:S(2)}) collective-permute-start(bf16[48,3,128]{2,0,1:T(8,128)(2,1)} %param.23), channel_id=1, source_target_pairs={{0,2},{2,0},{4,6},{6,4},{8,10},{10,8},{12,14},{14,12},{16,18},{18,... | collective-permute-start | bytes 110600 | tf_op jit(solution)/shard_map/ppermute | solution.py:15
  3.7 0.8 %select_reduce_fusion = (f32[48]{0:T(128)S(1)}, f32[48]{0:T(128)S(1)}) fusion(f32[16]{0:T(128)} %param.22, s32[48]{0:T(128)} %param.20, f32[16]{0:T(128)} %param.21), kind=kLoop, calls=%fused_computation.120 | loop fusion | flops 3744 | bytes 704 | tf_op jit(solution)/shard_map/reduce_sum | solution.py:81
  4.5 0.7 copy-done.3
  5.2 0.1 collective-permute-start.2
  5.3 0.6 copy-done.1
  5.9 1.6 %collective-permute-start = (f32[5,96]{1,0:T(8,128)S(1)}, f32[5,96]{1,0:T(8,128)S(1)}, u32[]{:S(2)}, u32[]{:S(2)}) collective-permute-start(f32[5,96]{1,0:T(8,128)S(1)} %pad_maximum_fusion.5), channel_id=1, source_target_pairs={{0,8},{2,10},{4,12},{6,14},{8,0},{10,2},{12,4},{14,6},{16,24},{18,... | collective-permute-start | bytes 5768 | tf_op jit(solution)/shard_map/ppermute | solution.py:15
  7.5 1.4 %collective-permute-done.2 = f32[7,48]{1,0:T(8,128)S(1)} collective-permute-done((f32[7,48]{1,0:T(8,128)S(1)}, f32[7,48]{1,0:T(8,128)S(1)}, u32[]{:S(2)}, u32[]{:S(2)}) %collective-permute-start.2) | collective-permute-done | bytes 1376 | tf_op jit(solution)/shard_map/ppermute | solution.py:15
  8.9 0.1 pad_maximum_fusion.6
  9.0 1.5 %collective-permute-start.3 = (f32[7,96]{1,0:T(8,128)S(1)}, f32[7,96]{1,0:T(8,128)S(1)}, u32[]{:S(2)}, u32[]{:S(2)}) collective-permute-start(f32[7,96]{1,0:T(8,128)S(1)} %pad_maximum_fusion.6), channel_id=1, source_target_pairs={{0,4},{2,6},{4,0},{6,2},{8,12},{10,14},{12,8},{14,10},{16,20},{18,... | collective-permute-start | bytes 8072 | tf_op jit(solution)/shard_map/ppermute | solution.py:15
  10.6 2.6 %collective-permute-start.1 = (f32[5,192]{1,0:T(8,128)S(1)}, f32[5,192]{1,0:T(8,128)S(1)}, u32[]{:S(2)}, u32[]{:S(2)}) collective-permute-start(f32[5,192]{1,0:T(8,128)S(1)} %pad_maximum_fusion.4), channel_id=1, source_target_pairs={{0,16},{2,18},{4,20},{6,22},{8,24},{10,26},{12,28},{14,30},{16,0},... | collective-permute-start | bytes 11528 | tf_op jit(solution)/shard_map/ppermute | solution.py:15
  13.2 0.1 multiply_bitcast_fusion
  13.3 0.1 multiply_bitcast_fusion.1
  13.5 1.6 %collective-permute-done.1 = f32[5,192]{1,0:T(8,128)S(1)} collective-permute-done((f32[5,192]{1,0:T(8,128)S(1)}, f32[5,192]{1,0:T(8,128)S(1)}, u32[]{:S(2)}, u32[]{:S(2)}) %collective-permute-start.1) | collective-permute-done | bytes 3872 | tf_op jit(solution)/shard_map/ppermute | solution.py:15
  15.2 0.7 collective-permute-start.5
  16.0 0.1 reshape.2726
  16.0 3.6 %collective-permute-done.5 = bf16[96,3,128]{2,0,1:T(8,128)(2,1)S(1)} collective-permute-done((bf16[96,3,128]{2,0,1:T(8,128)(2,1)S(1)}, bf16[96,3,128]{2,0,1:T(8,128)(2,1)S(1)}, u32[]{:S(2)}, u32[]{:S(2)}) %collective-permute-start.5) | collective-permute-done | bytes 73760 | tf_op jit(solution)/shard_map/ppermute | solution.py:15
  19.7 3.4 %while.11 = (s32[]{:T(128)}, f32[4,96,128]{2,1,0:T(8,128)S(1)}, f32[4,5,96]{2,0,1:T(4,128)S(1)}, f32[7,192]{1,0:T(8,128)S(1)}, f32[192,1]{0,1:T(1,128)S(1)}, /*i...) while((s32[]{:T(128)}, f32[4,96,128]{2,1,0:T(8,128)S(1)}, ...), condition=%wide.region_3.4_spmd, body=%wide.region_2.3_spmd.sunk | while | flops 16626054 | bytes 485213 | solution.py:173
  19.8 0.5 fusion.98
  20.3 0.2 fusion.99
  20.6 0.5 fusion.98
  21.2 0.2 fusion.99
  21.5 0.5 fusion.98
  22.0 0.2 fusion.99
  22.3 0.5 fusion.98
  22.9 0.2 fusion.99
  23.1 2.7 %collective-permute-start.6 = (f32[192,128]{1,0:T(8,128)S(1)}, f32[192,128]{1,0:T(8,128)S(1)}, u32[]{:S(2)}, u32[]{:S(2)}) collective-permute-start(f32[192,128]{1,0:T(8,128)S(1)} %bitcast.102), channel_id=1, source_target_pairs={{0,16},{2,18},{4,20},{6,22},{8,24},{10,26},{12,28},{14,30},{16,0},... | collective-permute-start | bytes 294920 | tf_op jit(solution)/shard_map/ppermute | solution.py:15
  25.8 2.9 %collective-permute-done.6 = f32[192,128]{1,0:T(8,128)S(1)} collective-permute-done((f32[192,128]{1,0:T(8,128)S(1)}, f32[192,128]{1,0:T(8,128)S(1)}, u32[]{:S(2)}, u32[]{:S(2)}) %collective-permute-start.6) | collective-permute-done | bytes 98336 | tf_op jit(solution)/shard_map/ppermute | solution.py:15
  28.8 2.2 %collective-permute-start.7 = (f32[96,128]{1,0:T(8,128)S(1)}, f32[96,128]{1,0:T(8,128)S(1)}, u32[]{:S(2)}, u32[]{:S(2)}) collective-permute-start(f32[96,128]{1,0:T(8,128)S(1)} %slice_select_fusion.2), channel_id=1, source_target_pairs={{0,8},{2,10},{4,12},{6,14},{8,0},{10,2},{12,4},{14,6},{16,24},{18,... | collective-permute-start | bytes 147464 | tf_op jit(solution)/shard_map/ppermute | solution.py:15
  31.0 2.1 %collective-permute-done.7 = f32[96,128]{1,0:T(8,128)S(1)} collective-permute-done((f32[96,128]{1,0:T(8,128)S(1)}, f32[96,128]{1,0:T(8,128)S(1)}, u32[]{:S(2)}, u32[]{:S(2)}) %collective-permute-start.7) | collective-permute-done | bytes 49184 | tf_op jit(solution)/shard_map/ppermute | solution.py:15
  33.0 0.7 multiply_reduce_fusion
  33.8 39.8 %psum.7 = f32[128]{0:T(128)S(1)} all-reduce(f32[128]{0:T(128)S(1)} %get-tuple-element.127), channel_id=1, replica_groups=mesh['patch'=16,'pix'=2] {'patch','pix'}, use_global_device_ids=true, to_apply=%region_5.6 | all-reduce | flops 128 | bytes 1024 | tf_op jit(solution)/shard_map/psum | solution.py:187
  73.6 0.5 broadcast_multiply_fusion.2
  (49 shorter events, 0.8 us)
Async XLA Ops:
  0.6 14.6 %collective-permute-start.4 = (bf16[48,3,128]{2,0,1:T(8,128)(2,1)}, bf16[48,3,128]{2,0,1:T(8,128)(2,1)S(1)}, u32[]{:S(2)}, u32[]{:S(2)}) collective-permute-start(bf16[48,3,128]{2,0,1:T(8,128)(2,1)} %param.23), channel_id=1, source_target_pairs={{0,2},{2,0},{4,6},{6,4},{8,10},{10,8},{12,14},{14,12},{16,18},{18,... | collective-permute-start | bytes 110600 | tf_op jit(solution)/shard_map/ppermute | solution.py:15
  4.5 0.7 copy-start.3
  4.5 0.7 copy-start.6
  5.2 0.7 copy-start.1
  5.2 0.7 copy-start.2
  5.2 3.7 %collective-permute-start.2 = (f32[7,48]{1,0:T(8,128)S(1)}, f32[7,48]{1,0:T(8,128)S(1)}, u32[]{:S(2)}, u32[]{:S(2)}) collective-permute-start(f32[7,48]{1,0:T(8,128)S(1)} %stack.24), channel_id=1, source_target_pairs={{0,2},{2,0},{4,6},{6,4},{8,10},{10,8},{12,14},{14,12},{16,18},{18,... | collective-permute-start | bytes 4040 | tf_op jit(solution)/shard_map/ppermute | solution.py:15
  5.9 4.6 %collective-permute-start = (f32[5,96]{1,0:T(8,128)S(1)}, f32[5,96]{1,0:T(8,128)S(1)}, u32[]{:S(2)}, u32[]{:S(2)}) collective-permute-start(f32[5,96]{1,0:T(8,128)S(1)} %pad_maximum_fusion.5), channel_id=1, source_target_pairs={{0,8},{2,10},{4,12},{6,14},{8,0},{10,2},{12,4},{14,6},{16,24},{18,... | collective-permute-start | bytes 5768 | tf_op jit(solution)/shard_map/ppermute | solution.py:15
  9.0 4.2 %collective-permute-start.3 = (f32[7,96]{1,0:T(8,128)S(1)}, f32[7,96]{1,0:T(8,128)S(1)}, u32[]{:S(2)}, u32[]{:S(2)}) collective-permute-start(f32[7,96]{1,0:T(8,128)S(1)} %pad_maximum_fusion.6), channel_id=1, source_target_pairs={{0,4},{2,6},{4,0},{6,2},{8,12},{10,14},{12,8},{14,10},{16,20},{18,... | collective-permute-start | bytes 8072 | tf_op jit(solution)/shard_map/ppermute | solution.py:15
  10.6 4.6 %collective-permute-start.1 = (f32[5,192]{1,0:T(8,128)S(1)}, f32[5,192]{1,0:T(8,128)S(1)}, u32[]{:S(2)}, u32[]{:S(2)}) collective-permute-start(f32[5,192]{1,0:T(8,128)S(1)} %pad_maximum_fusion.4), channel_id=1, source_target_pairs={{0,16},{2,18},{4,20},{6,22},{8,24},{10,26},{12,28},{14,30},{16,0},... | collective-permute-start | bytes 11528 | tf_op jit(solution)/shard_map/ppermute | solution.py:15
  13.3 1.9 %copy-start = (bf16[48,3,128]{2,0,1:T(8,128)(2,1)S(1)}, bf16[48,3,128]{2,0,1:T(8,128)(2,1)}, u32[]{:S(2)}) copy-start(bf16[48,3,128]{2,0,1:T(8,128)(2,1)} %param.23) | copy-start | bytes 110596
  15.2 4.4 %collective-permute-start.5 = (bf16[96,3,128]{2,0,1:T(8,128)(2,1)S(1)}, bf16[96,3,128]{2,0,1:T(8,128)(2,1)S(1)}, u32[]{:S(2)}, u32[]{:S(2)}) collective-permute-start(bf16[96,3,128]{2,0,1:T(8,128)(2,1)S(1)} %pad_maximum_fusion.1), channel_id=1, source_target_pairs={{0,4},{2,6},{4,0},{6,2},{8,12},{10,14},{12,8},{14,10},{16,20},{18,... | collective-permute-start | bytes 221192 | tf_op jit(solution)/shard_map/ppermute | solution.py:15
  23.1 5.6 %collective-permute-start.6 = (f32[192,128]{1,0:T(8,128)S(1)}, f32[192,128]{1,0:T(8,128)S(1)}, u32[]{:S(2)}, u32[]{:S(2)}) collective-permute-start(f32[192,128]{1,0:T(8,128)S(1)} %bitcast.102), channel_id=1, source_target_pairs={{0,16},{2,18},{4,20},{6,22},{8,24},{10,26},{12,28},{14,30},{16,0},... | collective-permute-start | bytes 294920 | tf_op jit(solution)/shard_map/ppermute | solution.py:15
  28.7 2.2 %copy-start.7 = (s32[96]{0:T(128)S(1)}, s32[96]{0:T(128)}, u32[]{:S(2)}) copy-start(s32[96]{0:T(128)} %param.17) | copy-start | bytes 1156
  28.8 4.3 %copy-start.4 = (f32[96]{0:T(128)S(1)}, f32[96]{0:T(128)}, u32[]{:S(2)}) copy-start(f32[96]{0:T(128)} %param.16) | copy-start | bytes 1156
  28.8 4.2 %copy-start.5 = (f32[96]{0:T(128)S(1)}, f32[96]{0:T(128)}, u32[]{:S(2)}) copy-start(f32[96]{0:T(128)} %param.15) | copy-start | bytes 1156
  28.8 4.2 %collective-permute-start.7 = (f32[96,128]{1,0:T(8,128)S(1)}, f32[96,128]{1,0:T(8,128)S(1)}, u32[]{:S(2)}, u32[]{:S(2)}) collective-permute-start(f32[96,128]{1,0:T(8,128)S(1)} %slice_select_fusion.2), channel_id=1, source_target_pairs={{0,8},{2,10},{4,12},{6,14},{8,0},{10,2},{12,4},{14,6},{16,24},{18,... | collective-permute-start | bytes 147464 | tf_op jit(solution)/shard_map/ppermute | solution.py:15
where the time goes:
time: 74.4 us; the launch traced here: 74.1 us
  blocking collectives  39.8 us (53%)
  starting transfers between devices  14.3 us (19%)
  waiting for transfers between devices  11.6 us (16%)
  other arithmetic  4.89 us (7%)
  local copies, waits for them, and re-layouts  1.55 us (2%)
  matrix products  0.95 us (1%)
  between operations  0.75 us (1%)
    psum x1, blocking collectives, per_device(): misfit = lax.psum(own_sum, ('patch', 'pix')) / pixels  39.8 us
    ppermute x8, starting transfers between devices, partner(): return lax.ppermute(value, axis, pairs)  14.3 us
    ppermute x8, waiting for transfers between devices, partner(): return lax.ppermute(value, axis, pairs)  11.6 us
    another operation x4, other arithmetic  2.11 us
  transfers between devices with their start and end apart: 8, of which 5 were waited for; matrix products, arithmetic and copies ran while one was open for 2% of the time, Pallas kernels for 0%

commit v1 on v0

v1 whole, which is shorter than its diff:
```python
import functools
import math

import jax
import jax.numpy as jnp
from jax import lax
from jax.experimental import pallas as pl
from jax.experimental.pallas import tpu as pltpu
from jax.sharding import PartitionSpec as P

MESH = pl.DeviceIdType.MESH
inv_two_pi = 1.0 / (2.0 * math.pi)
mu_ratio = 0.5
LANES = 128


def green_rows(sites, columns):
    src_east, src_north, depth, sin_s, cos_s, sin_d, cos_d = columns
    view_up = sites[4:5]
    east = sites[0:1] - src_east
    north = sites[1:2] - src_north
    x = east * sin_s + north * cos_s
    y = north * sin_s - east * cos_s
    view_x = sites[2:3] * sin_s + sites[3:4] * cos_s
    view_y = sites[3:4] * sin_s - sites[2:3] * cos_s
    p = y * cos_d + depth * sin_d
    q = y * sin_d - depth * cos_d
    xx = x * x
    yy = y * y
    rr = xx + yy + depth * depth
    over_r = lax.rsqrt(rr)
    radius = rr * over_r
    over_rd = 1.0 / (radius + depth)
    a = over_r * over_rd
    aa = a * a
    base = a * over_rd
    cubic = (3.0 * radius + depth) * (aa * a)
    square = (2.0 * radius + depth) * (aa * over_r)
    over_r2 = over_r * over_r
    over_r3 = over_r2 * over_r
    one = y * (base - xx * cubic)
    two = x * (base - yy * cubic)
    three = x * over_r3 - two
    four = x * y * square
    five = a - xx * square
    look = x * view_x + y * view_y + depth * view_up
    t = 3.0 * q * (over_r3 * over_r2) * look
    line_one = one * view_x + two * view_y - four * view_up
    line_two = three * view_x + one * view_y + five * view_up
    half_sin = mu_ratio * sin_d
    return (
        -(t * x + half_sin * line_one),
        half_sin * cos_d * line_two - t * p,
        t * q - half_sin * sin_d * line_two,
    )


def kernel(
    n,
    sites_ref,
    frames_ref,
    slip_ref,
    stats_ref,
    residual_ref,
    misfit_ref,
    sites_in,
    frames_in,
    slips_in,
    acc,
    part_in,
    sums_in,
    group_send,
    fwd_send,
    recv_sem,
    pair_send,
    pair_recv,
    sums_send,
    sums_recv,
):
    me = lax.axis_index("patch")
    core = lax.axis_index("pix")
    half = n // 2
    count = 2 * n
    rank = me * 2 + core
    parity = lax.rem(me, 2)
    place = me // 2
    across = me + 1 - 2 * parity
    sibling = 1 - core
    width = slip_ref.shape[0] // 3

    barrier = pltpu.get_barrier_semaphore()

    @pl.loop(1, count)
    def _(t):
        peer = lax.rem(rank + t, count)
        pl.semaphore_signal(
            barrier, inc=1, device_id=(peer // 2, lax.rem(peer, 2)), device_id_type=MESH
        )

    pl.semaphore_wait(barrier, count - 1)

    def remote(src, dst, send, recv, target):
        return pltpu.make_async_remote_copy(
            src_ref=src,
            dst_ref=dst,
            send_sem=send,
            recv_sem=recv,
            device_id=target,
            device_id_type=MESH,
        )

    def block_copies(frames, slip, slot, sends, step, target):
        return (
            remote(frames, frames_in.at[slot], sends.at[0, step], recv_sem.at[0, slot], target),
            remote(slip, slips_in.at[slot], sends.at[1, step], recv_sem.at[1, slot], target),
        )

    def group_member(t):
        return parity + 2 * lax.rem(place + t, half)

    own_across = block_copies(frames_ref, slip_ref, me, fwd_send, 0, (across, core))
    sites_copy = remote(sites_ref, sites_in, pair_send.at[0], pair_recv.at[0], (me, sibling))
    sites_copy.start()
    for copy in own_across:
        copy.start()

    @pl.loop(1, half)
    def _(t):
        for copy in block_copies(frames_ref, slip_ref, me, group_send, t, (group_member(t), core)):
            copy.start()

    acc[...] = jnp.zeros_like(acc)
    sites_copy.wait_recv()

    def add_source(frames, slip):
        turned = frames.T
        columns = [turned[:width, k : k + 1] for k in range(7)]
        for side, ref in enumerate((sites_ref, sites_in)):
            rows = jnp.concatenate(green_rows(ref[...], columns), axis=0)
            acc[side] += lax.dot_general(
                slip,
                rows.astype(jnp.bfloat16),
                (((0,), (0,)), ((), ())),
                preferred_element_type=jnp.float32,
            )

    add_source(frames_ref[...], slip_ref[...])

    @pl.loop(1, half)
    def _(t):
        source = group_member(half - t)
        incoming = block_copies(frames_ref, slip_ref, source, group_send, t, (across, core))
        onward = block_copies(
            frames_in.at[source], slips_in.at[source], source, fwd_send, t, (across, core)
        )
        for get, put in zip(incoming, onward):
            get.wait_recv()
            put.start()
        add_source(frames_in[source], slips_in[source])

    @pl.loop(0, half)
    def _(t):
        source = 1 - parity + 2 * lax.rem(place + half - t, half)
        for get in block_copies(frames_ref, slip_ref, source, group_send, 0, (across, core)):
            get.wait_recv()
        add_source(frames_in[source], slips_in[source])

    part_copy = remote(acc.at[1], part_in, pair_send.at[1], pair_recv.at[1], (me, sibling))
    part_copy.start()
    part_copy.wait_recv()
    observed, noise, valid = stats_ref[0:1], stats_ref[1:2], stats_ref[2:3]
    scaled = valid * (acc[0] + part_in[...] - observed) / noise
    residual = scaled.T[: residual_ref.shape[0]]
    sums_in[rank] = jnp.sum(residual * residual, axis=0, keepdims=True)

    @pl.loop(1, count)
    def _(t):
        peer = lax.rem(rank + t, count)
        remote(
            sums_in.at[rank],
            sums_in.at[rank],
            sums_send.at[t],
            sums_recv.at[rank],
            (peer // 2, lax.rem(peer, 2)),
        ).start()

    residual_ref[...] = residual

    sites_copy.wait_send()
    part_copy.wait_send()
    for copy in own_across:
        copy.wait_send()

    @pl.loop(1, half)
    def _(t):
        for copy in block_copies(frames_ref, slip_ref, me, group_send, t, (group_member(t), core)):
            copy.wait_send()
        source = group_member(half - t)
        for copy in block_copies(
            frames_in.at[source], slips_in.at[source], source, fwd_send, t, (across, core)
        ):
            copy.wait_send()

    @pl.loop(1, count)
    def _(t):
        peer = lax.rem(rank + t, count)
        target = (peer // 2, lax.rem(peer, 2))
        remote(
            sums_in.at[rank], sums_in.at[rank], sums_send.at[t], sums_recv.at[rank], target
        ).wait_send()
        remote(
            sums_in.at[rank], sums_in.at[peer], sums_send.at[t], sums_recv.at[peer], target
        ).wait_recv()

    pixels = residual_ref.shape[0] * count
    misfit_ref[...] = jnp.sum(sums_in[...], axis=0) / pixels


def padded(rows):
    table = jnp.stack(rows, axis=0)
    return jnp.pad(table, ((0, 8 - table.shape[0]), (0, LANES - table.shape[1])))


def per_device(
    n,
    pixel_pos,
    pixel_view,
    observed,
    noise_scale,
    valid_mask,
    patch_pos,
    patch_depth,
    segment_ids,
    seg_strike,
    seg_dip,
    slip_models,
):
    own_pixels = pixel_pos.shape[1]
    samples = slip_models.shape[2]
    width = slip_models.shape[0] // 2
    start = lax.axis_index("pix") * width
    view = pixel_view * inv_two_pi
    sites = padded([pixel_pos[0], pixel_pos[1], view[0], view[1], view[2]])
    mask = valid_mask.astype(jnp.float32)
    stats = jnp.pad(
        jnp.stack([observed, noise_scale, mask], axis=0), ((0, 5), (0, LANES - own_pixels))
    )
    stats = stats.at[1, own_pixels:].set(1.0)
    segments = seg_strike.shape[0]
    matches = segment_ids[:, None] == jnp.arange(segments, dtype=jnp.int32)[None, :]
    strike = jnp.sum(jnp.where(matches, seg_strike[None, :], 0.0), axis=1)
    dip = jnp.sum(jnp.where(matches, seg_dip[None, :], 0.0), axis=1)
    rows = [patch_pos[0], patch_pos[1], patch_depth]
    rows += [jnp.sin(strike), jnp.cos(strike), jnp.sin(dip), jnp.cos(dip)]
    frames = lax.dynamic_slice_in_dim(jnp.stack(rows, axis=0), start, width, axis=1)
    frames = jnp.pad(frames, ((0, 1), (0, LANES - width)))
    slip = lax.dynamic_slice_in_dim(slip_models, start, width, axis=0)
    slip = slip.transpose(1, 0, 2).reshape(3 * width, samples)
    half = n // 2
    vmem = pl.BlockSpec(memory_space=pltpu.VMEM)
    residual, misfit = pl.pallas_call(
        functools.partial(kernel, n),
        out_shape=(
            jax.ShapeDtypeStruct((own_pixels, samples), jnp.float32),
            jax.ShapeDtypeStruct((1, samples), jnp.float32),
        ),
        in_specs=[vmem] * 4,
        out_specs=(vmem, vmem),
        scratch_shapes=[
            pltpu.VMEM((8, LANES), jnp.float32),
            pltpu.VMEM((n, 8, LANES), jnp.float32),
            pltpu.VMEM((n, 3 * width, samples), jnp.bfloat16),
            pltpu.VMEM((2, samples, LANES), jnp.float32),
            pltpu.VMEM((samples, LANES), jnp.float32),
            pltpu.VMEM((2 * n, 1, samples), jnp.float32),
            pltpu.SemaphoreType.DMA((2, half)),
            pltpu.SemaphoreType.DMA((2, half)),
            pltpu.SemaphoreType.DMA((2, n)),
            pltpu.SemaphoreType.DMA((2,)),
            pltpu.SemaphoreType.DMA((2,)),
            pltpu.SemaphoreType.DMA((2 * n,)),
            pltpu.SemaphoreType.DMA((2 * n,)),
        ],
        compiler_params=pltpu.CompilerParams(collective_id=0, has_side_effects=True),
    )(sites, frames, slip, stats)
    return residual, misfit.reshape(samples)


def solution(mesh):
    return jax.shard_map(
        functools.partial(per_device, mesh.shape["patch"]),
        mesh=mesh,
        in_specs=(
            P(None, ("patch", "pix")),
            P(None, ("patch", "pix")),
            P(("patch", "pix")),
            P(("patch", "pix")),
            P(("patch", "pix")),
            P(None, "patch"),
            P("patch"),
            P("patch"),
            P(),
            P(),
            P("patch", None, None),
        ),
        out_specs=(P(("patch", "pix"), None), P()),
        check_vma=False,
    )
```

time: 74.4 us -> 33 us (0.44)
  blocking collectives: 39.8 us -> 0 us
  Pallas kernels: 0 us -> 24.8 us
  starting transfers between devices: 14.3 us -> 0 us
  waiting for transfers between devices: 11.6 us -> 0 us
  local copies, waits for them, and re-layouts: 1.55 us -> 6.44 us
  other arithmetic: 4.89 us -> 0.7 us
  matrix products: 0.95 us -> 0 us
    psum x1 -> x0, blocking collectives: 39.8 us -> none  [per_device(): misfit = lax.psum(own_sum, ('patch', 'pix')) / pixels]
    pallas_call x0 -> x1, Pallas kernels: none -> 24.8 us  [per_device(): pl.pallas_call(functools.partial(kernel, n), out_shape=(jax.ShapeDtypeStr...]
    ppermute x8 -> x0, starting transfers between devices: 14.3 us -> none  [partner(): return lax.ppermute(value, axis, pairs)]
    ppermute x8 -> x0, waiting for transfers between devices: 11.6 us -> none  [partner(): return lax.ppermute(value, axis, pairs)]
    unnamed x16 -> x28, local copies, waits for them, and re-layouts: 1.28 us -> 4.79 us
    another operation x4 -> x3, other arithmetic: 2.11 us -> 0.61 us  [the longest x1 0.59 us: padded(): table = jnp.stack(rows, axis=0)]
    reduce_sum x2 -> x1, other arithmetic: 1.5 us -> 0.09 us  [per_device(): dip = jnp.sum(jnp.where(matches, seg_dip[None, :], 0.0), axis=1)]
    dot_general x4 -> x0, matrix products: 0.95 us -> none  [tile_product(): lax.dot_general(green_tile, slip_table, (((0,), (0,)), ((), ())), preferr...]
  transfers between devices with their start and end apart: 8 -> 0, of which waited for: 5 -> 0; matrix products, arithmetic and copies ran while one was open for 2% -> 0% of each run, Pallas kernels for 0% -> 0%
where the time goes in v1:
time: 33 us; the launch traced here: 32.6 us
  Pallas kernels  24.8 us (75%)
  local copies, waits for them, and re-layouts  6.44 us (20%)
  between operations  0.73 us (2%)
  other arithmetic  0.7 us (2%)
    pallas_call x1, Pallas kernels, per_device(): pl.pallas_call(functools.partial(kernel, n), out_shape=(jax.ShapeDtypeStr...  24.8 us
    unnamed x28, local copies, waits for them, and re-layouts  4.79 us

profile of v1, /device:TPU:0, one launch (start us, length us, event | category | flops | bytes accessed | tf_op | source)
XLA Modules:
  0.0 32.6 jit_solution(2073114250455378153)
XLA Ops:
  0.6 0.0 copy-start
  0.7 0.0 copy-start.11
  0.7 0.6 %copy-done.11 = s32[96]{0:T(128)S(1)} copy-done((s32[96]{0:T(128)S(1)}, s32[96]{0:T(128)}, u32[]{:S(2)}) %copy-start.11) | copy-done | bytes 408
  1.3 0.0 copy-start.5
  1.3 0.0 copy-start.6
  1.3 0.0 copy-start.7
  1.3 0.6 %copy-done.5 = f32[16]{0:T(128)S(1)} copy-done((f32[16]{0:T(128)S(1)}, f32[16]{0:T(128)}, u32[]{:S(2)}) %copy-start.5) | copy-done | bytes 88
  2.0 0.0 copy-done.6
  2.0 0.0 copy-done.7
  2.0 0.1 select_reduce_fusion
  2.1 0.1 cosine_bitcast_fusion
  2.1 0.0 copy-start.3
  2.2 0.0 copy-start.10
  2.2 0.7 %copy-done.3 = f32[2,48]{1,0:T(2,128)S(1)} copy-done((f32[2,48]{1,0:T(2,128)S(1)}, f32[2,48]{1,0:T(2,128)}, u32[]{:S(2)}) %copy-start.3) | copy-done | bytes 408
  2.8 0.0 copy-done.10
  2.8 0.1 constant_dynamic-slice_fusion.1
  2.9 0.6 %pad.16.frames_ref = f32[8,128]{1,0:T(8,128)} pad(f32[7,24]{1,0:T(8,128)S(1)} %constant_dynamic-slice_fusion.1, f32[]{:T(128)} %constant.38.clone.1), padding=0_1x0_104 | pad | bytes 4772 | tf_op jit(solution)/shard_map/jit(_pad)/pad | solution.py:256
  3.5 0.1 copy-done.2
  3.6 0.7 %copy-done.4 = f32[2,96]{1,0:T(2,128)S(1)} copy-done((f32[2,96]{1,0:T(2,128)S(1)}, f32[2,96]{1,0:T(2,128)}, u32[]{:S(2)}) %copy-start.4) | copy-done | bytes 792
  4.3 0.6 %select_maximum_fusion.2.sites_ref = f32[8,128]{1,0:T(8,128)} fusion(f32[3,96]{1,0:T(4,128)S(1)} %broadcast_multiply_fusion, f32[2,96]{1,0:T(2,128)S(1)} %copy-done.4), kind=kLoop, calls=%fused_computation.6 | loop fusion | flops 8192 | bytes 6016 | tf_op jit(solution)/shard_map/stack | solution.py:220
  4.9 0.1 copy-done.8
  4.9 0.0 copy-done.9
  5.0 0.3 scatter.4.stats_ref
  5.3 0.0 copy-done
  5.3 0.0 copy-start.1
  5.3 0.6 %constant_dynamic-slice_fusion = bf16[24,3,128]{2,0,1:T(8,128)(2,1)} fusion(bf16[48,3,128]{2,0,1:T(8,128)(2,1)S(1)} %copy-done, s32[]{:T(128)S(6)} %select_n.13), kind=kLoop, calls=%fused_computation.11 | loop fusion | bytes 36868 | tf_op jit(solution)/shard_map/dynamic_slice | solution.py:257
  5.9 0.0 copy-done.1
  5.9 24.8 %shard_map.122 = (f32[96,128]{1,0:T(8,128)}, f32[1,128]{1,0:T(1,128)}) custom-call(f32[8,128]{1,0:T(8,128)} %select_maximum_fusion.2.sites_ref, f32[8,128]{1,0:T(8,128)} %pad.16.frames_ref, bf16[72,128]{1,0:T(8,128)(2,1)} %bitcast.17, f32[8,128]{1,0:T(8,128)} %copy-done.1), custom_call_target="tpu_custom_call" | custom-call | tf_op jit(solution)/shard_map/pallas_call | solution.py:261
  30.7 0.0 copy-start.12
  30.7 1.4 %copy.16 = f32[96,128]{1,0:T(8,128)} copy(f32[96,128]{1,0:T(8,128)} %get-tuple-element.28) | data formatting | bytes 98304
  32.1 0.0 copy-done.12
  32.1 0.5 %copy.17 = f32[128]{0:T(128)} copy(f32[128]{0:T(128)S(1)} %bitcast.21) | data formatting | bytes 1024
  (9 shorter events, 0.0 us)
Async XLA Ops:
  0.6 4.6 %copy-start = (bf16[48,3,128]{2,0,1:T(8,128)(2,1)S(1)}, bf16[48,3,128]{2,0,1:T(8,128)(2,1)}, u32[]{:S(2)}) copy-start(bf16[48,3,128]{2,0,1:T(8,128)(2,1)} %param.23) | copy-start | bytes 110596
  0.7 0.7 %copy-start.11 = (s32[96]{0:T(128)S(1)}, s32[96]{0:T(128)}, u32[]{:S(2)}) copy-start(s32[96]{0:T(128)} %param.17) | copy-start | bytes 1156
  1.3 0.7 %copy-start.5 = (f32[16]{0:T(128)S(1)}, f32[16]{0:T(128)}, u32[]{:S(2)}) copy-start(f32[16]{0:T(128)} %param.22) | copy-start | bytes 196
  1.3 0.7 %copy-start.6 = (s32[48]{0:T(128)S(1)}, s32[48]{0:T(128)}, u32[]{:S(2)}) copy-start(s32[48]{0:T(128)} %param.20) | copy-start | bytes 580
  1.3 0.7 %copy-start.7 = (f32[16]{0:T(128)S(1)}, f32[16]{0:T(128)}, u32[]{:S(2)}) copy-start(f32[16]{0:T(128)} %param.21) | copy-start | bytes 196
  2.1 0.7 %copy-start.3 = (f32[2,48]{1,0:T(2,128)S(1)}, f32[2,48]{1,0:T(2,128)}, u32[]{:S(2)}) copy-start(f32[2,48]{1,0:T(2,128)} %param.18) | copy-start | bytes 1156
  2.2 0.7 %copy-start.10 = (f32[48]{0:T(128)S(1)}, f32[48]{0:T(128)}, u32[]{:S(2)}) copy-start(f32[48]{0:T(128)} %param.19) | copy-start | bytes 580
  2.9 0.7 %copy-start.2 = (f32[3,96]{1,0:T(4,128)S(1)}, f32[3,96]{1,0:T(4,128)}, u32[]{:S(2)}) copy-start(f32[3,96]{1,0:T(4,128)} %param.14) | copy-start | bytes 3460
  3.6 0.7 %copy-start.4 = (f32[2,96]{1,0:T(2,128)S(1)}, f32[2,96]{1,0:T(2,128)}, u32[]{:S(2)}) copy-start(f32[2,96]{1,0:T(2,128)} %param.13) | copy-start | bytes 2308
  4.3 0.7 %copy-start.8 = (f32[96]{0:T(128)S(1)}, f32[96]{0:T(128)}, u32[]{:S(2)}) copy-start(f32[96]{0:T(128)} %param.16) | copy-start | bytes 1156
  4.3 0.7 %copy-start.9 = (f32[96]{0:T(128)S(1)}, f32[96]{0:T(128)}, u32[]{:S(2)}) copy-start(f32[96]{0:T(128)} %param.15) | copy-start | bytes 1156
  5.3 0.6 %copy-start.1 = (f32[8,128]{1,0:T(8,128)}, f32[8,128]{1,0:T(8,128)S(1)}, u32[]{:S(2)}) copy-start(f32[8,128]{1,0:T(8,128)S(1)} %scatter.4.stats_ref) | copy-start | bytes 12292
  30.7 1.4 %copy-start.12 = (f32[1,128]{1,0:T(1,128)S(1)}, f32[1,128]{1,0:T(1,128)}, u32[]{:S(2)}) copy-start(f32[1,128]{1,0:T(1,128)} %get-tuple-element.17) | copy-start | bytes 1540

commit v2 on v1

v2 whole, which is shorter than its diff:
```python
import functools
import math

import jax
import jax.numpy as jnp
from jax import lax
from jax.experimental import pallas as pl
from jax.experimental.pallas import tpu as pltpu
from jax.sharding import PartitionSpec as P

MESH = pl.DeviceIdType.MESH
inv_two_pi = 1.0 / (2.0 * math.pi)
mu_ratio = 0.5
LANES = 128


def green_rows(sites, columns):
    src_east, src_north, depth, sin_s, cos_s, sin_d, cos_d = columns
    view_up = sites[4:5]
    east = sites[0:1] - src_east
    north = sites[1:2] - src_north
    x = east * sin_s + north * cos_s
    y = north * sin_s - east * cos_s
    view_x = sites[2:3] * sin_s + sites[3:4] * cos_s
    view_y = sites[3:4] * sin_s - sites[2:3] * cos_s
    p = y * cos_d + depth * sin_d
    q = y * sin_d - depth * cos_d
    xx = x * x
    yy = y * y
    rr = xx + yy + depth * depth
    over_r = lax.rsqrt(rr)
    radius = rr * over_r
    over_rd = 1.0 / (radius + depth)
    a = over_r * over_rd
    aa = a * a
    base = a * over_rd
    cubic = (3.0 * radius + depth) * (aa * a)
    square = (2.0 * radius + depth) * (aa * over_r)
    over_r2 = over_r * over_r
    over_r3 = over_r2 * over_r
    one = y * (base - xx * cubic)
    two = x * (base - yy * cubic)
    three = x * over_r3 - two
    four = x * y * square
    five = a - xx * square
    look = x * view_x + y * view_y + depth * view_up
    t = 3.0 * q * (over_r3 * over_r2) * look
    line_one = one * view_x + two * view_y - four * view_up
    line_two = three * view_x + one * view_y + five * view_up
    half_sin = mu_ratio * sin_d
    return (
        -(t * x + half_sin * line_one),
        half_sin * cos_d * line_two - t * p,
        t * q - half_sin * sin_d * line_two,
    )


def frame_table(core, pos, depth, ids, strike, dip, width):
    segments = strike.shape[1]
    rows = lax.broadcasted_iota(jnp.int32, (segments, segments), 0)
    diagonal = rows == lax.broadcasted_iota(jnp.int32, (segments, segments), 1)
    matches = lax.broadcasted_iota(jnp.int32, (segments, ids.shape[1]), 0) == ids

    def lookup(row):
        column = jnp.sum(jnp.where(diagonal, row, 0.0), axis=1, keepdims=True)
        return jnp.sum(jnp.where(matches, column, 0.0), axis=0, keepdims=True)

    angles = jnp.concatenate([lookup(strike), lookup(dip)], axis=0)
    sines, cosines = jnp.sin(angles), jnp.cos(angles)
    table = jnp.concatenate([pos, depth, sines[0:1], cosines[0:1], sines[1:2], cosines[1:2]], axis=0)
    table = jnp.where(core == 1, table[:, width:], table[:, :width])
    table = jnp.concatenate([table, jnp.zeros((7, LANES // 4 - width), jnp.float32)], axis=1)
    spare = jnp.zeros((1, LANES // 4), jnp.float32)
    upper = jnp.concatenate([table[k : k + 1] for k in range(4)], axis=1)
    lower = jnp.concatenate([table[k : k + 1] for k in range(4, 7)] + [spare], axis=1)
    return jnp.concatenate([upper, lower], axis=0)


def kernel(
    n,
    *refs,
):
    args, refs = refs[:11], refs[11:]
    residual_ref, misfit_ref, refs = refs[0], refs[1], refs[2:]
    local, refs = refs[:11], refs[11:]
    (
        sites_own,
        sites_in,
        frames_in,
        slips_in,
        greens,
        acc,
        part_in,
        sums_in,
        load_sem,
        frames_send,
        frames_recv,
        group_send,
        fwd_send,
        slip_recv,
        pair_send,
        pair_recv,
        sums_send,
        sums_recv,
    ) = refs
    me = lax.axis_index("patch")
    core = lax.axis_index("pix")
    half = n // 2
    count = 2 * n
    rank = me * 2 + core
    parity = lax.rem(me, 2)
    place = me // 2
    across = me + 1 - 2 * parity
    sibling = 1 - core
    width = local[10].shape[1]
    pixels = residual_ref.shape[0]

    barrier = pltpu.get_barrier_semaphore()

    @pl.loop(1, count)
    def _(t):
        peer = lax.rem(rank + t, count)
        pl.semaphore_signal(
            barrier, inc=1, device_id=(peer // 2, lax.rem(peer, 2)), device_id_type=MESH
        )

    loads = []
    for k in range(11):
        src = args[k]
        if k == 10:
            src = src.at[:, pl.ds(pl.multiple_of(core * width, 8), width)]
        loads.append(pltpu.make_async_copy(src, local[k], load_sem.at[k]))
    for load in loads:
        load.start()
    for load in loads:
        load.wait()

    sites_own[...] = jnp.zeros_like(sites_own)
    sites_own[0:2, :pixels] = local[0][...]
    sites_own[2:5, :pixels] = local[1][...] * inv_two_pi
    frames_in[me] = frame_table(core, *[local[k][...] for k in range(5, 10)], width)
    slip = local[10][...].astype(jnp.float32)
    rows = [slip[k] for k in range(3)] + [jnp.zeros((8, slip.shape[2]), jnp.float32)]
    slips_in[0, place] = jnp.concatenate(rows, axis=0).astype(jnp.bfloat16)

    pl.semaphore_wait(barrier, count - 1)

    def remote(src, dst, send, recv, target):
        return pltpu.make_async_remote_copy(
            src_ref=src,
            dst_ref=dst,
            send_sem=send,
            recv_sem=recv,
            device_id=target,
            device_id_type=MESH,
        )

    def frames_copy(t):
        source, target = me, lax.rem(me + t, n)
        return remote(
            frames_in.at[source],
            frames_in.at[source],
            frames_send.at[t],
            frames_recv.at[source],
            (target, core),
        )

    def group_copy(t):
        target = parity + 2 * lax.rem(place + t, half)
        mine = slips_in.at[0, place]
        return remote(mine, mine, group_send.at[t], slip_recv.at[0, place], (target, core))

    def onward_copy(slot):
        return remote(
            slips_in.at[0, slot],
            slips_in.at[1, slot],
            fwd_send.at[slot],
            slip_recv.at[1, slot],
            (across, core),
        )

    def arrival(ref, sem):
        return remote(ref, ref, pair_send.at[0], sem, (across, core))

    sites_copy = remote(sites_own, sites_in, pair_send.at[0], pair_recv.at[0], (me, sibling))
    sites_copy.start()

    @pl.loop(1, n)
    def _(t):
        frames_copy(t).start()

    onward_copy(place).start()

    @pl.loop(1, half)
    def _(t):
        group_copy(t).start()

    def add_green(side, slot):
        source = 2 * slot + (parity if side == 0 else 1 - parity)
        turned = jnp.concatenate([frames_in[source], jnp.zeros((6, LANES), jnp.float32)], axis=0).T
        columns = []
        for k in range(7):
            base = (k % 4) * (LANES // 4)
            columns.append(turned[base : base + width, k // 4 : k // 4 + 1])
        for lane, ref in enumerate((sites_own, sites_in)):
            rows = green_rows(ref[...], columns) + (jnp.zeros((8, LANES), jnp.float32),)
            block = jnp.concatenate(rows, axis=0).astype(jnp.bfloat16)
            greens[side, slot, :, lane * LANES : (lane + 1) * LANES] = block

    def wait_frames(side, slot):
        source = 2 * slot + (parity if side == 0 else 1 - parity)
        arrival(frames_in.at[source], frames_recv.at[source]).wait_recv()

    sites_copy.wait_recv()
    add_green(0, place)

    @pl.loop(1, half)
    def _(t):
        slot = lax.rem(place + half - t, half)
        wait_frames(0, slot)
        add_green(0, slot)
        arrival(slips_in.at[0, slot], slip_recv.at[0, slot]).wait_recv()
        onward_copy(slot).start()
        wait_frames(1, slot)
        add_green(1, slot)

    wait_frames(1, place)
    add_green(1, place)

    chunk = math.gcd(half, 8)

    def product(side, step, lane):
        slips = slips_in[side, pl.ds(step * chunk, chunk)]
        block = greens[side, pl.ds(step * chunk, chunk), :, lane * LANES : (lane + 1) * LANES]
        return lax.dot_general(
            slips.reshape(-1, slips.shape[-1]),
            block.reshape(-1, LANES),
            (((0,), (0,)), ((), ())),
            preferred_element_type=jnp.float32,
        )

    acc[...] = jnp.zeros_like(acc)

    @pl.loop(0, half // chunk)
    def _(step):
        for lane in range(2):
            acc[lane] += product(0, step, lane)

    @pl.loop(0, half)
    def _(t):
        slot = lax.rem(place + half - t, half)
        arrival(slips_in.at[1, slot], slip_recv.at[1, slot]).wait_recv()

    @pl.loop(0, half // chunk)
    def _(step):
        acc[1] += product(1, step, 1)

    part_copy = remote(acc.at[1], part_in, pair_send.at[1], pair_recv.at[1], (me, sibling))
    part_copy.start()

    @pl.loop(0, half // chunk)
    def _(step):
        acc[0] += product(1, step, 0)

    valid = local[4][...].astype(jnp.float32)
    part_copy.wait_recv()
    total = (acc[0] + part_in[...])[:, :pixels]
    scaled = valid * (total - local[2][...]) / local[3][...]
    blank = jnp.zeros((total.shape[0], LANES - pixels), jnp.float32)
    residual = jnp.concatenate([scaled, blank], axis=1).T[:pixels]
    sums_in[rank] = jnp.sum(residual * residual, axis=0, keepdims=True)

    def sums_copy(t, slot):
        peer = lax.rem(rank + t, count)
        return remote(
            sums_in.at[slot],
            sums_in.at[slot],
            sums_send.at[t],
            sums_recv.at[slot],
            (peer // 2, lax.rem(peer, 2)),
        )

    @pl.loop(1, count)
    def _(t):
        sums_copy(t, rank).start()

    residual_ref[...] = residual
    sites_copy.wait_send()
    part_copy.wait_send()

    @pl.loop(1, n)
    def _(t):
        frames_copy(t).wait_send()

    @pl.loop(1, half)
    def _(t):
        group_copy(t).wait_send()

    @pl.loop(0, half)
    def _(slot):
        onward_copy(slot).wait_send()

    @pl.loop(1, count)
    def _(t):
        sums_copy(t, rank).wait_send()
        sums_copy(t, lax.rem(rank + t, count)).wait_recv()

    misfit_ref[...] = jnp.sum(sums_in[...], axis=0) / (pixels * count)


def per_device(n, *args):
    args = [arg.reshape(1, -1) if arg.ndim == 1 else arg for arg in args]
    args[10] = args[10].transpose(1, 0, 2)
    own_pixels = args[0].shape[1]
    width = args[10].shape[1] // 2
    samples = args[10].shape[2]
    half = n // 2
    vmem = pl.BlockSpec(memory_space=pltpu.VMEM)
    local = [pltpu.VMEM(arg.shape, arg.dtype) for arg in args[:10]]
    local.append(pltpu.VMEM((3, width, samples), jnp.bfloat16))
    depth = 3 * width + 8
    dma = pltpu.SemaphoreType.DMA
    residual, misfit = pl.pallas_call(
        functools.partial(kernel, n),
        out_shape=(
            pltpu.VMEM((own_pixels, samples), jnp.float32),
            pltpu.VMEM((1, samples), jnp.float32),
        ),
        in_specs=[pl.BlockSpec(memory_space=pl.ANY)] * 11,
        out_specs=(vmem, vmem),
        scratch_shapes=local
        + [
            pltpu.VMEM((8, LANES), jnp.float32),
            pltpu.VMEM((8, LANES), jnp.float32),
            pltpu.VMEM((n, 2, LANES), jnp.float32),
            pltpu.VMEM((2, half, depth, samples), jnp.bfloat16),
            pltpu.VMEM((2, half, depth, 2 * LANES), jnp.bfloat16),
            pltpu.VMEM((2, samples, LANES), jnp.float32),
            pltpu.VMEM((samples, LANES), jnp.float32),
            pltpu.VMEM((2 * n, 1, samples), jnp.float32),
            dma((11,)),
            dma((n,)),
            dma((n,)),
            dma((half,)),
            dma((half,)),
            dma((2, half)),
            dma((2,)),
            dma((2,)),
            dma((2 * n,)),
            dma((2 * n,)),
        ],
        compiler_params=pltpu.CompilerParams(collective_id=0, has_side_effects=True),
    )(*args)
    return residual, misfit.reshape(samples)


def solution(mesh):
    return jax.shard_map(
        functools.partial(per_device, mesh.shape["patch"]),
        mesh=mesh,
        in_specs=(
            P(None, ("patch", "pix")),
            P(None, ("patch", "pix")),
            P(("patch", "pix")),
            P(("patch", "pix")),
            P(("patch", "pix")),
            P(None, "patch"),
            P("patch"),
            P("patch"),
            P(),
            P(),
            P("patch", None, None),
        ),
        out_specs=(P(("patch", "pix"), None), P()),
        check_vma=False,
    )
```

time: 33 us -> 25.9 us (0.78)
  local copies, waits for them, and re-layouts: 6.44 us -> 1.13 us
  Pallas kernels: 24.8 us -> 23.9 us
  other arithmetic: 0.7 us -> 0 us
    unnamed x28 -> x2, local copies, waits for them, and re-layouts: 4.79 us -> 1.13 us
    pallas_call x1, Pallas kernels: 24.8 us -> 23.9 us  [per_device(): pl.pallas_call(functools.partial(kernel, n), out_shape=(pltpu.VMEM((own_p...]
    dynamic_slice x2 -> x0, local copies, waits for them, and re-layouts: 0.69 us -> none  [the longest x1 0.62 us: per_device(): slip = lax.dynamic_slice_in_dim(slip_models, start, width, axis=0)]
    another operation x3 -> x0, other arithmetic: 0.61 us -> none  [the longest x1 0.59 us: padded(): table = jnp.stack(rows, axis=0)]
    pad x1 -> x0, local copies, waits for them, and re-layouts: 0.6 us -> none  [per_device(): frames = jnp.pad(frames, ((0, 1), (0, LANES - width)))]
where the time goes in v2:
time: 25.9 us; the launch traced here: 25.7 us
  Pallas kernels  23.9 us (92%)
  local copies, waits for them, and re-layouts  1.13 us (4%)
  between operations  0.64 us (2%)
    pallas_call x1, Pallas kernels, per_device(): pl.pallas_call(functools.partial(kernel, n), out_shape=(pltpu.VMEM((own_p...  23.9 us
    unnamed x2, local copies, waits for them, and re-layouts  1.13 us

profile of v2, /device:TPU:0, one launch (start us, length us, event | category | flops | bytes accessed | tf_op | source)
XLA Modules:
  0.0 25.7 jit_solution(16319223729853142553)
XLA Ops:
  0.6 23.9 %shard_map.122 = (f32[96,128]{1,0:T(8,128)S(1)}, f32[1,128]{1,0:T(1,128)S(1)}) custom-call(f32[2,96]{1,0:T(2,128)} %refs_0_.1, f32[3,96]{1,0:T(4,128)} %refs_1_.1, f32[1,96]{1,0:T(1,128)} %bitcast.11, f32[1,96]{1,0:T(1,128)} %bitcast.12, s32[1,96]{1,0:T(1,128)} %bitcast.13, f32[2,48]{1,0:T(2,128)} %refs_5_.1, f32[1,48]{1,0:T(1,128)} %bitcast.14, ...), custom_call_target="tpu_custom_call" | custom-call | tf_op jit(solution)/shard_map/pallas_call | solution.py:323
  24.6 0.6 %copy.15 = f32[96,128]{1,0:T(8,128)} copy(f32[96,128]{1,0:T(8,128)S(1)} %get-tuple-element.6) | data formatting | bytes 98304
  25.2 0.5 %copy.16 = f32[128]{0:T(128)} copy(f32[128]{0:T(128)S(1)} %bitcast.9) | data formatting | bytes 1024

commit v3 on v2

--- a/solution.py
+++ b/solution.py
@@ -86,17 +86,14 @@
     (
         sites_own,
         sites_in,
-        frames_in,
         slips_in,
         greens,
         acc,
         part_in,
         sums_in,
         load_sem,
-        frames_send,
-        frames_recv,
-        group_send,
-        fwd_send,
+        line_send,
+        hop_send,
         slip_recv,
         pair_send,
         pair_recv,
@@ -105,24 +102,29 @@
     ) = refs
     me = lax.axis_index("patch")
     core = lax.axis_index("pix")
-    half = n // 2
+    line = n // 4
     count = 2 * n
     rank = me * 2 + core
-    parity = lax.rem(me, 2)
-    place = me // 2
-    across = me + 1 - 2 * parity
+    place = me // 4
+    across_x = me + 1 - 2 * lax.rem(me, 2)
+    across_y = me + 2 - 4 * lax.rem(me // 2, 2)
+    heading = 1 - 2 * (place // (line - line // 2))
     sibling = 1 - core
     width = local[10].shape[1]
     pixels = residual_ref.shape[0]
 
     barrier = pltpu.get_barrier_semaphore()
 
-    @pl.loop(1, count)
-    def _(t):
-        peer = lax.rem(rank + t, count)
-        pl.semaphore_signal(
-            barrier, inc=1, device_id=(peer // 2, lax.rem(peer, 2)), device_id_type=MESH
-        )
+    def greet(target):
+        pl.semaphore_signal(barrier, inc=1, device_id=target, device_id_type=MESH)
+
+    @pl.loop(1, line)
+    def _(t):
+        greet((lax.rem(me + 4 * t, n), core))
+
+    greet((across_x, core))
+    greet((across_y, core))
+    greet((me, sibling))
 
     loads = []
     for k in range(11):
@@ -138,12 +140,14 @@
     sites_own[...] = jnp.zeros_like(sites_own)
     sites_own[0:2, :pixels] = local[0][...]
     sites_own[2:5, :pixels] = local[1][...] * inv_two_pi
-    frames_in[me] = frame_table(core, *[local[k][...] for k in range(5, 10)], width)
+    frames = frame_table(core, *[local[k][...] for k in range(5, 10)], width)
+    high = frames.astype(jnp.bfloat16).astype(jnp.float32)
+    middle = (frames - high).astype(jnp.bfloat16).astype(jnp.float32)
     slip = local[10][...].astype(jnp.float32)
-    rows = [slip[k] for k in range(3)] + [jnp.zeros((8, slip.shape[2]), jnp.float32)]
+    rows = [slip[k] for k in range(3)] + [high, middle, frames - high - middle, 0.0 * high]
     slips_in[0, place] = jnp.concatenate(rows, axis=0).astype(jnp.bfloat16)
 
-    pl.semaphore_wait(barrier, count - 1)
+    pl.semaphore_wait(barrier, line + 2)
 
     def remote(src, dst, send, recv, target):
         return pltpu.make_async_remote_copy(
@@ -155,49 +159,49 @@
             device_id_type=MESH,
         )
 
-    def frames_copy(t):
-        source, target = me, lax.rem(me + t, n)
+    def line_copy(t):
+        mine = slips_in.at[0, place]
+        target = lax.rem(me + 4 * t, n)
+        return remote(mine, mine, line_send.at[t], slip_recv.at[0, place], (target, core))
+
+    def hop_copy(kind, quad, into, slot, target):
         return remote(
-            frames_in.at[source],
-            frames_in.at[source],
-            frames_send.at[t],
-            frames_recv.at[source],
+            slips_in.at[quad, slot],
+            slips_in.at[into, slot],
+            hop_send.at[kind, slot],
+            slip_recv.at[into, slot],
             (target, core),
         )
 
-    def group_copy(t):
-        target = parity + 2 * lax.rem(place + t, half)
-        mine = slips_in.at[0, place]
-        return remote(mine, mine, group_send.at[t], slip_recv.at[0, place], (target, core))
-
-    def onward_copy(slot):
-        return remote(
-            slips_in.at[0, slot],
-            slips_in.at[1, slot],
-            fwd_send.at[slot],
-            slip_recv.at[1, slot],
-            (across, core),
-        )
-
-    def arrival(ref, sem):
-        return remote(ref, ref, pair_send.at[0], sem, (across, core))
+    def side_copies(slot):
+        return (hop_copy(0, 0, 1, slot, across_y), hop_copy(1, 0, 2, slot, across_x))
+
+    def corner_copy(slot):
+        odd = lax.rem(slot, 2)
+        target = across_x + odd * (across_y - across_x)
+        return hop_copy(2, 1 + odd, 3, slot, target)
+
+    def wait_block(quad, slot):
+        ref, sem = slips_in.at[quad, slot], slip_recv.at[quad, slot]
+        remote(ref, ref, hop_send.at[0, slot], sem, (across_x, core)).wait_recv()
+
+    def slot_at(t):
+        return lax.rem(place + t * heading + line, line)
 
     sites_copy = remote(sites_own, sites_in, pair_send.at[0], pair_recv.at[0], (me, sibling))
+    for copy in side_copies(place):
+        copy.start()
+
+    @pl.loop(1, line)
+    def _(t):
+        line_copy(t).start()
+
     sites_copy.start()
 
-    @pl.loop(1, n)
-    def _(t):
-        frames_copy(t).start()
-
-    onward_copy(place).start()
-
-    @pl.loop(1, half)
-    def _(t):
-        group_copy(t).start()
-
-    def add_green(side, slot):
-        source = 2 * slot + (parity if side == 0 else 1 - parity)
-        turned = jnp.concatenate([frames_in[source], jnp.zeros((6, LANES), jnp.float32)], axis=0).T
+    def add_green(quad, slot):
+        packed = slips_in[quad, slot, 3 * width :, :].astype(jnp.float32)
+        frames = packed[0:2] + packed[2:4] + packed[4:6]
+        turned = jnp.concatenate([frames, jnp.zeros((6, LANES), jnp.float32)], axis=0).T
         columns = []
         for k in range(7):
             base = (k % 4) * (LANES // 4)
@@ -205,29 +209,36 @@
         for lane, ref in enumerate((sites_own, sites_in)):
             rows = green_rows(ref[...], columns) + (jnp.zeros((8, LANES), jnp.float32),)
             block = jnp.concatenate(rows, axis=0).astype(jnp.bfloat16)
-            greens[side, slot, :, lane * LANES : (lane + 1) * LANES] = block
-
-    def wait_frames(side, slot):
-        source = 2 * slot + (parity if side == 0 else 1 - parity)
-        arrival(frames_in.at[source], frames_recv.at[source]).wait_recv()
+            greens[quad, slot, :, lane * LANES : (lane + 1) * LANES] = block
+
+    def turn_corner(slot):
+        quad = 1 + lax.rem(slot, 2)
+        wait_block(quad, slot)
+        corner_copy(slot).start()
+        add_green(quad, slot)
 
     sites_copy.wait_recv()
     add_green(0, place)
 
-    @pl.loop(1, half)
-    def _(t):
-        slot = lax.rem(place + half - t, half)
-        wait_frames(0, slot)
+    @pl.loop(1, line)
+    def _(t):
+        slot = slot_at(t)
+        wait_block(0, slot)
+        for copy in side_copies(slot):
+            copy.start()
         add_green(0, slot)
-        arrival(slips_in.at[0, slot], slip_recv.at[0, slot]).wait_recv()
-        onward_copy(slot).start()
-        wait_frames(1, slot)
-        add_green(1, slot)
-
-    wait_frames(1, place)
-    add_green(1, place)
-
-    chunk = math.gcd(half, 8)
+        turn_corner(slot_at(t - 1))
+
+    turn_corner(slot_at(line - 1))
+
+    @pl.loop(0, line)
+    def _(t):
+        slot = slot_at(t)
+        quad = 2 - lax.rem(slot, 2)
+        wait_block(quad, slot)
+        add_green(quad, slot)
+
+    chunk = math.gcd(line, 8)
 
     def product(side, step, lane):
         slips = slips_in[side, pl.ds(step * chunk, chunk)]
@@ -241,26 +252,28 @@
 
     acc[...] = jnp.zeros_like(acc)
 
-    @pl.loop(0, half // chunk)
+    @pl.loop(0, line // chunk)
     def _(step):
         for lane in range(2):
-            acc[lane] += product(0, step, lane)
-
-    @pl.loop(0, half)
-    def _(t):
-        slot = lax.rem(place + half - t, half)
-        arrival(slips_in.at[1, slot], slip_recv.at[1, slot]).wait_recv()
-
-    @pl.loop(0, half // chunk)
+            for quad in range(3):
+                acc[lane] += product(quad, step, lane)
+
+    @pl.loop(0, line)
+    def _(t):
+        slot = slot_at(t)
+        wait_block(3, slot)
+        add_green(3, slot)
+
+    @pl.loop(0, line // chunk)
     def _(step):
-        acc[1] += product(1, step, 1)
+        acc[1] += product(3, step, 1)
 
     part_copy = remote(acc.at[1], part_in, pair_send.at[1], pair_recv.at[1], (me, sibling))
     part_copy.start()
 
-    @pl.loop(0, half // chunk)
+    @pl.loop(0, line // chunk)
     def _(step):
-        acc[0] += product(1, step, 0)
+        acc[0] += product(3, step, 0)
 
     valid = local[4][...].astype(jnp.float32)
     part_copy.wait_recv()
@@ -288,17 +301,15 @@
     sites_copy.wait_send()
     part_copy.wait_send()
 
-    @pl.loop(1, n)
-    def _(t):
-        frames_copy(t).wait_send()
-
-    @pl.loop(1, half)
-    def _(t):
-        group_copy(t).wait_send()
-
-    @pl.loop(0, half)
+    @pl.loop(1, line)
+    def _(t):
+        line_copy(t).wait_send()
+
+    @pl.loop(0, line)
     def _(slot):
-        onward_copy(slot).wait_send()
+        for copy in side_copies(slot):
+            copy.wait_send()
+        corner_copy(slot).wait_send()
 
     @pl.loop(1, count)
     def _(t):
@@ -314,7 +325,7 @@
     own_pixels = args[0].shape[1]
     width = args[10].shape[1] // 2
     samples = args[10].shape[2]
-    half = n // 2
+    line = n // 4
     vmem = pl.BlockSpec(memory_space=pltpu.VMEM)
     local = [pltpu.VMEM(arg.shape, arg.dtype) for arg in args[:10]]
     local.append(pltpu.VMEM((3, width, samples), jnp.bfloat16))
@@ -332,18 +343,15 @@
         + [
             pltpu.VMEM((8, LANES), jnp.float32),
             pltpu.VMEM((8, LANES), jnp.float32),
-            pltpu.VMEM((n, 2, LANES), jnp.float32),
-            pltpu.VMEM((2, half, depth, samples), jnp.bfloat16),
-            pltpu.VMEM((2, half, depth, 2 * LANES), jnp.bfloat16),
+            pltpu.VMEM((4, line, depth, samples), jnp.bfloat16),
+            pltpu.VMEM((4, line, depth, 2 * LANES), jnp.bfloat16),
             pltpu.VMEM((2, samples, LANES), jnp.float32),
             pltpu.VMEM((samples, LANES), jnp.float32),
             pltpu.VMEM((2 * n, 1, samples), jnp.float32),
             dma((11,)),
-            dma((n,)),
-            dma((n,)),
-            dma((half,)),
-            dma((half,)),
-            dma((2, half)),
+            dma((line,)),
+            dma((3, line)),
+            dma((4, line)),
             dma((2,)),
             dma((2,)),
             dma((2 * n,)),

time: 25.9 us -> 25.4 us (0.981)
  Pallas kernels: 23.9 us -> 23.5 us
    pallas_call x1, Pallas kernels: 23.9 us -> 23.5 us  [per_device(): pl.pallas_call(functools.partial(kernel, n), out_shape=(pltpu.VMEM((own_p...]
where the time goes in v3:
time: 25.4 us; the launch traced here: 25.2 us
  Pallas kernels  23.5 us (93%)
  local copies, waits for them, and re-layouts  1.13 us (4%)
  between operations  0.64 us (3%)
    pallas_call x1, Pallas kernels, per_device(): pl.pallas_call(functools.partial(kernel, n), out_shape=(pltpu.VMEM((own_p...  23.5 us
    unnamed x2, local copies, waits for them, and re-layouts  1.13 us

profile of v3, /device:TPU:0, one launch (start us, length us, event | category | flops | bytes accessed | tf_op | source)
XLA Modules:
  0.0 25.2 jit_solution(9961524213804713842)
XLA Ops:
  0.6 23.5 %shard_map.122 = (f32[96,128]{1,0:T(8,128)S(1)}, f32[1,128]{1,0:T(1,128)S(1)}) custom-call(f32[2,96]{1,0:T(2,128)} %refs_0_.1, f32[3,96]{1,0:T(4,128)} %refs_1_.1, f32[1,96]{1,0:T(1,128)} %bitcast.11, f32[1,96]{1,0:T(1,128)} %bitcast.12, s32[1,96]{1,0:T(1,128)} %bitcast.13, f32[2,48]{1,0:T(2,128)} %refs_5_.1, f32[1,48]{1,0:T(1,128)} %bitcast.14, ...), custom_call_target="tpu_custom_call" | custom-call | tf_op jit(solution)/shard_map/pallas_call | solution.py:334
  24.1 0.6 %copy.15 = f32[96,128]{1,0:T(8,128)} copy(f32[96,128]{1,0:T(8,128)S(1)} %get-tuple-element.6) | data formatting | bytes 98304
  24.7 0.5 %copy.16 = f32[128]{0:T(128)} copy(f32[128]{0:T(128)S(1)} %bitcast.9) | data formatting | bytes 1024
